TPU v7x, 32 devices: a whole 2x2x4 slice. The times are simulated.
32 devices in a mesh: dp: 4 (over z), feat: 8 (over y, x, core).
Axes of the slice: x: 2, y: 2, z: 4, core: 2. Of those that a mesh axis runs over, the one named last changes fastest.
Arguments:
- features: float32 [4096, 8192], P('dp', 'feat'), may hold values from -0.0625 to 0.0625
- labels: int32 [4096], P('dp'), may hold values from -1 to 1, as said below
- weights: float32 [8192], P('feat'), may hold values from -6 to 6
Outputs:
- gradient: float32 [8192], P('feat')
- newton_step: float32 [8192], P('feat')
- residual: float32 [8192], P('feat')
Inputs may be any that keep to these rules, and one draw needn't show every extreme that they name: `labels`: every label is -1 or +1.
All inputs are finite; a program needn't handle non-finite values.
Results may differ from a plain program's by a relative error of at most 0.0003.
Values sent between devices are 32-bit elements; how exact they have to be, the bound alone decides.
A program may use at most 64 MiB of HBM per device.

v0:
```python
import jax
import jax.numpy as jnp
from jax import lax
from jax.sharding import PartitionSpec as P

CG_STEPS = 3
PENALTY = 4.0
HIGH = lax.Precision.HIGHEST


def squares(residual):
    return lax.psum(jnp.sum(residual * residual), "feat")


def local(features, labels, weights):
    y = labels.astype(jnp.float32)
    margin = y * lax.psum(jnp.dot(features, weights, precision=HIGH), "feat")
    sig = 1.0 / (1.0 + jnp.exp(-margin))
    local_grad = jnp.dot((sig - 1.0) * y, features, precision=HIGH)
    gradient = weights + PENALTY * lax.psum(local_grad, "dp")
    curv = PENALTY * sig * (1.0 - sig)
    newton_step = jnp.zeros_like(weights)
    residual = -gradient
    direction = residual
    rr = squares(residual)
    for step in range(CG_STEPS):
        image_rows, dir_sq = lax.psum(
            (jnp.dot(features, direction, precision=HIGH), jnp.sum(direction * direction)), "feat"
        )
        weighted = curv * image_rows
        back, quad = lax.psum(
            (jnp.dot(weighted, features, precision=HIGH), jnp.sum(weighted * image_rows)), "dp"
        )
        curvature = dir_sq + quad
        image = direction + back
        alpha = rr / curvature
        newton_step = newton_step + alpha * direction
        residual = residual - alpha * image
        fresh = squares(residual)
        direction = residual + fresh / rr * direction
        rr = fresh
    return (gradient, newton_step, residual)


def solution(mesh):
    placed = (P("dp", "feat"), P("dp"), P("feat"))
    return jax.shard_map(
        local,
        mesh=mesh,
        in_specs=placed,
        out_specs=(P("feat"), P("feat"), P("feat")),
        check_vma=False,
    )
```

profile of v0, /device:TPU:0, one launch (start us, length us, event | category | flops | bytes accessed | tf_op | source)
XLA Modules:
  0.0 174.1 jit_solution(13997829717275814949)
XLA Ops:
  0.6 0.0 copy-start.2
  0.6 0.0 copy-start.1
  0.7 5.8 %fusion.3 = f32[1,1024]{1,0:T(1,128)S(1)} fusion(f32[1024,1024]{1,0:T(8,128)} %param.3, f32[1024,1]{0,1:T(1,128)} %bitcast.34), kind=kOutput, calls=%fused_computation.21 | convolution fusion | flops 12582912 | bytes 4202496 | tf_op jit(solution)/shard_map/dot_general | solution.py:17
  6.4 15.2 %psum.115 = f32[1024]{0:T(1024)S(1)} all-reduce(f32[1024]{0:T(1024)S(1)} %bitcast.45), channel_id=1, replica_groups=mesh['dp'=4,'feat'=8] {'feat'}, use_global_device_ids=true, to_apply=%region_0.0 | all-reduce | flops 1024 | bytes 8192 | tf_op jit(solution)/shard_map/psum | solution.py:17
  21.6 0.0 copy-done.2
  21.6 4.3 %fusion.4 = f32[1,1024]{1,0:T(1,128)S(1)} fusion(f32[1024,1]{0,1:T(1,128)S(1)} %bitcast.47, f32[1024,1024]{1,0:T(8,128)} %param.3), kind=kOutput, calls=%fused_computation.22 | convolution fusion | flops 12582912 | bytes 4202496 | tf_op jit(solution)/shard_map/dot_general | solution.py:19
  25.9 11.9 %psum.116 = f32[1024]{0:T(1024)S(1)} all-reduce(f32[1024]{0:T(1024)S(1)} %bitcast.44), channel_id=1, replica_groups=mesh['dp'=4,'feat'=8] {'dp'}, use_global_device_ids=true, to_apply=%region_1.0 | all-reduce | flops 1024 | bytes 8192 | tf_op jit(solution)/shard_map/psum | solution.py:20
  37.8 0.0 copy-done.1
  37.8 0.6 multiply_reduce_fusion.7
  38.4 5.6 %fusion.5 = f32[1,1024]{1,0:T(1,128)S(1)} fusion(f32[1024,1]{0,1:T(1,128)S(1)} %bitcast.46, f32[1024,1024]{1,0:T(8,128)} %param.3), kind=kOutput, calls=%fused_computation.23 | convolution fusion | flops 12582912 | bytes 4202496 | tf_op jit(solution)/shard_map/dot_general | solution.py:28
  44.1 12.8 %all-reduce.2 = (f32[1024]{0:T(1024)S(1)}, f32[]{:T(128)}) all-reduce(f32[1024]{0:T(1024)S(1)} %bitcast.38, f32[]{:T(128)} %get-tuple-element.21), channel_id=1, replica_groups=mesh['dp'=4,'feat'=8] {'feat'}, use_global_device_ids=true, to_apply=%region_4.0 | all-reduce | flops 1025 | bytes 8200 | tf_op jit(solution)/shard_map/psum | solution.py:27
  56.8 0.6 multiply_reduce_fusion.6
  57.4 4.3 %fusion.6 = f32[1,1024]{1,0:T(1,128)S(1)} fusion(f32[1024,1]{0,1:T(1,128)S(1)} %bitcast.36, f32[1024,1024]{1,0:T(8,128)} %param.3), kind=kOutput, calls=%fused_computation.24 | convolution fusion | flops 12582912 | bytes 4202496 | tf_op jit(solution)/shard_map/dot_general | solution.py:32
  61.7 9.1 %all-reduce.5 = (f32[1024]{0:T(1024)S(1)}, f32[]{:T(128)}) all-reduce(f32[1024]{0:T(1024)S(1)} %bitcast.39, f32[]{:T(128)} %get-tuple-element.29), channel_id=1, replica_groups=mesh['dp'=4,'feat'=8] {'dp'}, use_global_device_ids=true, to_apply=%region_7.0 | all-reduce | flops 1025 | bytes 8200 | tf_op jit(solution)/shard_map/psum | solution.py:31
  72.7 0.6 multiply_reduce_fusion.5
  73.3 12.6 %psum.121 = f32[]{:T(128)} all-reduce(f32[]{:T(128)} %multiply_reduce_fusion.5), channel_id=1, replica_groups=mesh['dp'=4,'feat'=8] {'feat'}, use_global_device_ids=true, to_apply=%region_9.0 | all-reduce | flops 1 | bytes 8 | tf_op jit(solution)/shard_map/psum | solution.py:12
  87.3 0.6 multiply_reduce_fusion.4
  87.9 5.6 %fusion.7 = f32[1,1024]{1,0:T(1,128)S(1)} fusion(f32[1024,1]{0,1:T(1,128)S(1)} %bitcast.32, f32[1024,1024]{1,0:T(8,128)} %param.3), kind=kOutput, calls=%fused_computation.25 | convolution fusion | flops 12582912 | bytes 4202496 | tf_op jit(solution)/shard_map/dot_general | solution.py:28
  93.5 12.8 %all-reduce.1 = (f32[1024]{0:T(1024)S(1)}, f32[]{:T(128)}) all-reduce(f32[1024]{0:T(1024)S(1)} %bitcast.42, f32[]{:T(128)} %get-tuple-element.19), channel_id=1, replica_groups=mesh['dp'=4,'feat'=8] {'feat'}, use_global_device_ids=true, to_apply=%region_12.0 | all-reduce | flops 1025 | bytes 8200 | tf_op jit(solution)/shard_map/psum | solution.py:27
  106.3 0.7 multiply_reduce_fusion.3
  107.0 4.3 %fusion.8 = f32[1,1024]{1,0:T(1,128)S(1)} fusion(f32[1024,1]{0,1:T(1,128)S(1)} %bitcast.37, f32[1024,1024]{1,0:T(8,128)} %param.3), kind=kOutput, calls=%fused_computation.26 | convolution fusion | flops 12582912 | bytes 4202496 | tf_op jit(solution)/shard_map/dot_general | solution.py:32
  111.2 11.1 %all-reduce.4 = (f32[1024]{0:T(1024)S(1)}, f32[]{:T(128)}) all-reduce(f32[1024]{0:T(1024)S(1)} %bitcast.40, f32[]{:T(128)} %get-tuple-element.27), channel_id=1, replica_groups=mesh['dp'=4,'feat'=8] {'dp'}, use_global_device_ids=true, to_apply=%region_15.0 | all-reduce | flops 1025 | bytes 8200 | tf_op jit(solution)/shard_map/psum | solution.py:31
  124.2 0.6 multiply_reduce_fusion.2
  124.8 12.4 %psum.126 = f32[]{:T(128)} all-reduce(f32[]{:T(128)} %get-tuple-element.17), channel_id=1, replica_groups=mesh['dp'=4,'feat'=8] {'feat'}, use_global_device_ids=true, to_apply=%region_17.0 | all-reduce | flops 1 | bytes 8 | tf_op jit(solution)/shard_map/psum | solution.py:12
  138.6 0.6 multiply_reduce_fusion.1
  139.2 5.6 %fusion.9 = f32[1,1024]{1,0:T(1,128)S(1)} fusion(f32[1024,1]{0,1:T(1,128)S(1)} %bitcast.33, f32[1024,1024]{1,0:T(8,128)} %param.3), kind=kOutput, calls=%fused_computation.27 | convolution fusion | flops 12582912 | bytes 4202496 | tf_op jit(solution)/shard_map/dot_general | solution.py:28
  144.8 12.7 %all-reduce = (f32[]{:T(128)}, f32[1024]{0:T(1024)S(1)}) all-reduce(f32[]{:T(128)} %get-tuple-element.15, f32[1024]{0:T(1024)S(1)} %bitcast.43), channel_id=1, replica_groups=mesh['dp'=4,'feat'=8] {'feat'}, use_global_device_ids=true, to_apply=%region_19.0 | all-reduce | flops 1025 | bytes 8200 | tf_op jit(solution)/shard_map/psum | solution.py:27
  157.6 0.7 fusion
  158.3 4.3 %fusion.10 = f32[1,1024]{1,0:T(1,128)S(1)} fusion(f32[1024,1]{0,1:T(1,128)S(1)} %bitcast.35, f32[1024,1024]{1,0:T(8,128)} %param.3), kind=kOutput, calls=%fused_computation.28 | convolution fusion | flops 12582912 | bytes 4202496 | tf_op jit(solution)/shard_map/dot_general | solution.py:32
  162.5 9.1 %all-reduce.3 = (f32[]{:T(128)}, f32[1024]{0:T(1024)S(1)}) all-reduce(f32[]{:T(128)} %get-tuple-element.26, f32[1024]{0:T(1024)S(1)} %bitcast.41), channel_id=1, replica_groups=mesh['dp'=4,'feat'=8] {'dp'}, use_global_device_ids=true, to_apply=%region_22.0 | all-reduce | flops 1025 | bytes 8200 | tf_op jit(solution)/shard_map/psum | solution.py:31
  173.5 0.0 copy-done
  173.5 0.6 multiply_subtract_fusion
  (3 shorter events, 0.0 us)
Async XLA Ops:
  0.6 20.9 %copy-start.2 = (s32[1024]{0:T(1024)S(1)}, s32[1024]{0:T(1024)}, u32[]{:S(2)}) copy-start(s32[1024]{0:T(1024)} %param.4) | copy-start | bytes 12292
  0.6 37.2 %copy-start.1 = (f32[1024]{0:T(1024)S(1)}, f32[1024]{0:T(1024)}, u32[]{:S(2)}) copy-start(f32[1024]{0:T(1024)} %param.5) | copy-start | bytes 12292
  38.4 135.1 %copy-start = (f32[1024]{0:T(1024)}, f32[1024]{0:T(1024)S(1)}, u32[]{:S(2)}) copy-start(f32[1024]{0:T(1024)S(1)} %get-tuple-element.22) | copy-start | bytes 12292
where the time goes:
time: 175 us; the launch traced here: 174 us
  blocking collectives  120 us (69%)
  matrix products  39.8 us (23%)
  between operations  9.03 us (5%)
  other arithmetic  5.6 us (3%)
    psum x3, blocking collectives, local(): lax.psum((jnp.dot(features, direction, precision=HIGH), jnp.sum(direction...  38.2 us
    psum x3, blocking collectives, local(): lax.psum((jnp.dot(weighted, features, precision=HIGH), jnp.sum(weighted *...  29.4 us
    psum x2, blocking collectives, squares(): return lax.psum(jnp.sum(residual * residual), 'feat')  25 us
    dot_general x3, matrix products, local(): jnp.dot(features, direction, precision=HIGH)  16.9 us
    psum x1, blocking collectives, local(): margin = y * lax.psum(jnp.dot(features, weights, precision=HIGH), 'feat')  15.2 us
    dot_general x3, matrix products, local(): jnp.dot(weighted, features, precision=HIGH)  12.8 us
    psum x1, blocking collectives, local(): gradient = weights + PENALTY * lax.psum(local_grad, 'dp')  11.9 us
    dot_general x1, matrix products, local(): margin = y * lax.psum(jnp.dot(features, weights, precision=HIGH), 'feat')  5.76 us

commit v1 on v0

--- a/solution.py
+++ b/solution.py
@@ -6,6 +6,12 @@
 CG_STEPS = 3
 PENALTY = 4.0
 HIGH = lax.Precision.HIGHEST
+
+
+def add_all(x, mesh_axis):
+    terms = lax.all_gather(x, mesh_axis, axis=0, tiled=False)
+    summed = terms.sum(axis=0)
+    return summed
 
 
 def squares(residual):
@@ -17,7 +23,7 @@
     margin = y * lax.psum(jnp.dot(features, weights, precision=HIGH), "feat")
     sig = 1.0 / (1.0 + jnp.exp(-margin))
     local_grad = jnp.dot((sig - 1.0) * y, features, precision=HIGH)
-    gradient = weights + PENALTY * lax.psum(local_grad, "dp")
+    gradient = weights + PENALTY * add_all(local_grad, "dp")
     curv = PENALTY * sig * (1.0 - sig)
     newton_step = jnp.zeros_like(weights)
     residual = -gradient

time: 175 us -> 180 us (1.029)
  blocking collectives: 120 us -> 125 us
    all_gather x0 -> x1, blocking collectives: none -> 13.4 us  [add_all(): terms = lax.all_gather(x, mesh_axis, axis=0, tiled=False)]
    psum x1 -> x0, blocking collectives: 11.9 us -> none  [local(): gradient = weights + PENALTY * lax.psum(local_grad, 'dp')]
    psum x3, blocking collectives: 29.4 us -> 32.8 us  [local(): lax.psum((jnp.dot(weighted, features, precision=HIGH), jnp.sum(weighted *...]
where the time goes in v1:
time: 180 us; the launch traced here: 179 us
  blocking collectives  125 us (69%)
  matrix products  39.8 us (22%)
  between operations  9.04 us (5%)
  other arithmetic  5.62 us (3%)
    psum x3, blocking collectives, local(): lax.psum((jnp.dot(features, direction, precision=HIGH), jnp.sum(direction...  38.2 us
    psum x3, blocking collectives, local(): lax.psum((jnp.dot(weighted, features, precision=HIGH), jnp.sum(weighted *...  32.8 us
    psum x2, blocking collectives, squares(): return lax.psum(jnp.sum(residual * residual), 'feat')  25 us
    dot_general x3, matrix products, local(): jnp.dot(features, direction, precision=HIGH)  16.9 us
    psum x1, blocking collectives, local(): margin = y * lax.psum(jnp.dot(features, weights, precision=HIGH), 'feat')  15.2 us
    all_gather x1, blocking collectives, add_all(): terms = lax.all_gather(x, mesh_axis, axis=0, tiled=False)  13.4 us
    dot_general x3, matrix products, local(): jnp.dot(weighted, features, precision=HIGH)  12.8 us
    dot_general x1, matrix products, local(): margin = y * lax.psum(jnp.dot(features, weights, precision=HIGH), 'feat')  5.76 us

profile of v1, /device:TPU:0, one launch (start us, length us, event | category | flops | bytes accessed | tf_op | source)
XLA Modules:
  0.0 179.1 jit_solution(14512712680258148531)
XLA Ops:
  0.6 0.0 copy-start.2
  0.6 0.0 copy-start.1
  0.7 5.8 %fusion.3 = f32[1,1024]{1,0:T(1,128)S(1)} fusion(f32[1024,1024]{1,0:T(8,128)} %param.3, f32[1024,1]{0,1:T(1,128)} %bitcast.34), kind=kOutput, calls=%fused_computation.21 | convolution fusion | flops 12582912 | bytes 4202496 | tf_op jit(solution)/shard_map/dot_general | solution.py:23
  6.4 15.2 %psum.108 = f32[1024]{0:T(1024)S(1)} all-reduce(f32[1024]{0:T(1024)S(1)} %bitcast.45), channel_id=1, replica_groups=mesh['dp'=4,'feat'=8] {'feat'}, use_global_device_ids=true, to_apply=%region_0.0 | all-reduce | flops 1024 | bytes 8192 | tf_op jit(solution)/shard_map/psum | solution.py:23
  21.6 0.0 copy-done.2
  21.6 4.3 %fusion.4 = f32[1,1024]{1,0:T(1,128)S(1)} fusion(f32[1024,1]{0,1:T(1,128)S(1)} %bitcast.47, f32[1024,1024]{1,0:T(8,128)} %param.3), kind=kOutput, calls=%fused_computation.22 | convolution fusion | flops 12582912 | bytes 4202496 | tf_op jit(solution)/shard_map/dot_general | solution.py:25
  25.9 13.4 %all-gather = f32[4096]{0:T(1024)S(1)} all-gather(f32[1024]{0:T(1024)S(1)} %bitcast.38), channel_id=2, replica_groups=mesh['dp'=4,'feat'=8] {'dp'}, dimensions={0}, use_global_device_ids=true | all-gather | bytes 20480 | tf_op jit(solution)/shard_map/all_gather | solution.py:12
  39.3 0.0 copy-done.1
  39.3 0.6 multiply_reduce_fusion.7
  39.9 5.6 %fusion.5 = f32[1,1024]{1,0:T(1,128)S(1)} fusion(f32[1024,1]{0,1:T(1,128)S(1)} %bitcast.46, f32[1024,1024]{1,0:T(8,128)} %param.3), kind=kOutput, calls=%fused_computation.23 | convolution fusion | flops 12582912 | bytes 4202496 | tf_op jit(solution)/shard_map/dot_general | solution.py:34
  45.6 12.8 %all-reduce.2 = (f32[1024]{0:T(1024)S(1)}, f32[]{:T(128)}) all-reduce(f32[1024]{0:T(1024)S(1)} %bitcast.39, f32[]{:T(128)} %get-tuple-element.21), channel_id=1, replica_groups=mesh['dp'=4,'feat'=8] {'feat'}, use_global_device_ids=true, to_apply=%region_4.0 | all-reduce | flops 1025 | bytes 8200 | tf_op jit(solution)/shard_map/psum | solution.py:33
  58.3 0.6 multiply_reduce_fusion.6
  58.9 4.3 %fusion.6 = f32[1,1024]{1,0:T(1,128)S(1)} fusion(f32[1024,1]{0,1:T(1,128)S(1)} %bitcast.36, f32[1024,1024]{1,0:T(8,128)} %param.3), kind=kOutput, calls=%fused_computation.24 | convolution fusion | flops 12582912 | bytes 4202496 | tf_op jit(solution)/shard_map/dot_general | solution.py:38
  63.2 12.6 %all-reduce.5 = (f32[1024]{0:T(1024)S(1)}, f32[]{:T(128)}) all-reduce(f32[1024]{0:T(1024)S(1)} %bitcast.40, f32[]{:T(128)} %get-tuple-element.29), channel_id=1, replica_groups=mesh['dp'=4,'feat'=8] {'dp'}, use_global_device_ids=true, to_apply=%region_7.0 | all-reduce | flops 1025 | bytes 8200 | tf_op jit(solution)/shard_map/psum | solution.py:37
  77.7 0.6 multiply_reduce_fusion.5
  78.4 12.6 %psum.113 = f32[]{:T(128)} all-reduce(f32[]{:T(128)} %multiply_reduce_fusion.5), channel_id=1, replica_groups=mesh['dp'=4,'feat'=8] {'feat'}, use_global_device_ids=true, to_apply=%region_9.0 | all-reduce | flops 1 | bytes 8 | tf_op jit(solution)/shard_map/psum | solution.py:18
  92.3 0.6 multiply_reduce_fusion.4
  92.9 5.6 %fusion.7 = f32[1,1024]{1,0:T(1,128)S(1)} fusion(f32[1024,1]{0,1:T(1,128)S(1)} %bitcast.32, f32[1024,1024]{1,0:T(8,128)} %param.3), kind=kOutput, calls=%fused_computation.25 | convolution fusion | flops 12582912 | bytes 4202496 | tf_op jit(solution)/shard_map/dot_general | solution.py:34
  98.5 12.8 %all-reduce.1 = (f32[1024]{0:T(1024)S(1)}, f32[]{:T(128)}) all-reduce(f32[1024]{0:T(1024)S(1)} %bitcast.43, f32[]{:T(128)} %get-tuple-element.19), channel_id=1, replica_groups=mesh['dp'=4,'feat'=8] {'feat'}, use_global_device_ids=true, to_apply=%region_12.0 | all-reduce | flops 1025 | bytes 8200 | tf_op jit(solution)/shard_map/psum | solution.py:33
  111.3 0.7 multiply_reduce_fusion.3
  112.0 4.3 %fusion.8 = f32[1,1024]{1,0:T(1,128)S(1)} fusion(f32[1024,1]{0,1:T(1,128)S(1)} %bitcast.37, f32[1024,1024]{1,0:T(8,128)} %param.3), kind=kOutput, calls=%fused_computation.26 | convolution fusion | flops 12582912 | bytes 4202496 | tf_op jit(solution)/shard_map/dot_general | solution.py:38
  116.2 9.1 %all-reduce.4 = (f32[1024]{0:T(1024)S(1)}, f32[]{:T(128)}) all-reduce(f32[1024]{0:T(1024)S(1)} %bitcast.41, f32[]{:T(128)} %get-tuple-element.27), channel_id=1, replica_groups=mesh['dp'=4,'feat'=8] {'dp'}, use_global_device_ids=true, to_apply=%region_15.0 | all-reduce | flops 1025 | bytes 8200 | tf_op jit(solution)/shard_map/psum | solution.py:37
  127.2 0.6 multiply_reduce_fusion.2
  127.8 12.4 %psum.118 = f32[]{:T(128)} all-reduce(f32[]{:T(128)} %get-tuple-element.17), channel_id=1, replica_groups=mesh['dp'=4,'feat'=8] {'feat'}, use_global_device_ids=true, to_apply=%region_17.0 | all-reduce | flops 1 | bytes 8 | tf_op jit(solution)/shard_map/psum | solution.py:18
  141.6 0.6 multiply_reduce_fusion.1
  142.2 5.6 %fusion.9 = f32[1,1024]{1,0:T(1,128)S(1)} fusion(f32[1024,1]{0,1:T(1,128)S(1)} %bitcast.33, f32[1024,1024]{1,0:T(8,128)} %param.3), kind=kOutput, calls=%fused_computation.27 | convolution fusion | flops 12582912 | bytes 4202496 | tf_op jit(solution)/shard_map/dot_general | solution.py:34
  147.8 12.7 %all-reduce = (f32[]{:T(128)}, f32[1024]{0:T(1024)S(1)}) all-reduce(f32[]{:T(128)} %get-tuple-element.15, f32[1024]{0:T(1024)S(1)} %bitcast.44), channel_id=1, replica_groups=mesh['dp'=4,'feat'=8] {'feat'}, use_global_device_ids=true, to_apply=%region_19.0 | all-reduce | flops 1025 | bytes 8200 | tf_op jit(solution)/shard_map/psum | solution.py:33
  160.6 0.7 fusion
  161.2 4.3 %fusion.10 = f32[1,1024]{1,0:T(1,128)S(1)} fusion(f32[1024,1]{0,1:T(1,128)S(1)} %bitcast.35, f32[1024,1024]{1,0:T(8,128)} %param.3), kind=kOutput, calls=%fused_computation.28 | convolution fusion | flops 12582912 | bytes 4202496 | tf_op jit(solution)/shard_map/dot_general | solution.py:38
  165.5 11.1 %all-reduce.3 = (f32[]{:T(128)}, f32[1024]{0:T(1024)S(1)}) all-reduce(f32[]{:T(128)} %get-tuple-element.26, f32[1024]{0:T(1024)S(1)} %bitcast.42), channel_id=1, replica_groups=mesh['dp'=4,'feat'=8] {'dp'}, use_global_device_ids=true, to_apply=%region_22.0 | all-reduce | flops 1025 | bytes 8200 | tf_op jit(solution)/shard_map/psum | solution.py:37
  178.5 0.0 copy-done
  178.5 0.6 multiply_subtract_fusion
  (5 shorter events, 0.0 us)
Async XLA Ops:
  0.6 20.9 %copy-start.2 = (s32[1024]{0:T(1024)S(1)}, s32[1024]{0:T(1024)}, u32[]{:S(2)}) copy-start(s32[1024]{0:T(1024)} %param.4) | copy-start | bytes 12292
  0.6 38.7 %copy-start.1 = (f32[1024]{0:T(1024)S(1)}, f32[1024]{0:T(1024)}, u32[]{:S(2)}) copy-start(f32[1024]{0:T(1024)} %param.5) | copy-start | bytes 12292
  39.9 138.6 %copy-start = (f32[1024]{0:T(1024)}, f32[1024]{0:T(1024)S(1)}, u32[]{:S(2)}) copy-start(f32[1024]{0:T(1024)S(1)} %get-tuple-element.22) | copy-start | bytes 12292
